TPU v7x, 512 devices: a whole 4x4x16 slice. The times are simulated.
512 devices in a mesh: tm: 128 (over z, x, y_hi), chan: 4 (over y_lo, core).
Axes of the slice: x: 4, y: 4 (y_hi: 2, y_lo: 2; y = y_hi * 2 + y_lo), z: 16, core: 2. Of those that a mesh axis runs over, the one named last changes fastest.
Arguments:
- frames: bfloat16 [65536, 1024], P('tm', 'chan'), may hold values from -6 to 6
- w_in: bfloat16 [3, 1024, 1024], P(None, None, 'chan'), may hold values from -0.1875 to 0.1875
- short_taps: float32 [3, 3, 1024], P(None, None, 'chan'), may hold values from -3 to 3
- filter_taps: bfloat16 [65536, 1024], P('tm', 'chan'), may hold values from -0.0234375 to 0.0234375
- skip_gain: float32 [1024], P('chan'), may hold values from -4 to 4
- w_out: bfloat16 [1024, 1024], P(None, 'chan'), may hold values from -0.1875 to 0.1875
Outputs:
- layer_out: bfloat16 [65536, 1024], P('tm', 'chan')
All inputs are finite; a program needn't handle non-finite values.
Results may differ from a plain program's by a relative error of at most 0.011.
Values may be sent and summed in bfloat16 or wider, within the bound.
A program may use at most 64 MiB of HBM per device.

v0:
```python
import functools

import jax
import jax.numpy as jnp
import numpy as np
from jax import lax
from jax.experimental import pallas as pl
from jax.experimental.pallas import tpu as pltpu
from jax.sharding import PartitionSpec as P

MESH = pl.DeviceIdType.MESH
ROWS = 128
COLS = 512
CHANS = 256
PEERS = ROWS - 1
LANES = 128
HALO = 16
F32 = jnp.float32
BF16 = jnp.bfloat16


def tables():
    r = np.arange(ROWS, dtype=np.int64)
    k = np.arange(ROWS, dtype=np.int64)
    c = np.arange(COLS, dtype=np.int64)
    row = (2.0 * np.pi / (4 * ROWS)) * ((r[None, :] * (4 * k[:, None] + 1)) % (4 * ROWS))
    turn = (2.0 * np.pi / (4 * ROWS * COLS)) * (c[None, :] * (4 * k[:, None] + 1))
    col = (2.0 * np.pi / COLS) * ((c[:, None] * c[None, :]) % COLS)
    row_both = np.concatenate([np.cos(row), -np.sin(row)], axis=0)
    return (
        jnp.asarray(row_both, BF16),
        jnp.asarray(row_both.T, BF16),
        jnp.asarray(np.cos(turn), F32),
        jnp.asarray(np.sin(turn), F32),
        jnp.asarray(np.cos(col), BF16),
        jnp.asarray(np.sin(col), BF16),
    )


def dot(left, right):
    return jnp.dot(left, right, preferred_element_type=F32)


def kernel(
    frames_h, filt_h, taps_h, skip_h, w_in_h, w_out_h, row_h, rowi_h, tc_h, ts_h, cc_h, cs_h,
    out,
    taps, skip, w_in, w_out, row, rowi, tcos, tsin, ccos, csin,
    xg, filt, p, qf, sf, slab, fsend, frecv, ssend, srecv, csend, crecv,
    gbuf, gg, gmat, q2, spec, xm, ym, bstack, acc,
    load_sem, wout_sem, over_s, over_r, near_s, near_r, pass_s, pass_r,
    gover_s, gover_r, gnear_s, gnear_r, gpass_s, gpass_r, a_s, a_r, h_s, h_r,
):
    t = lax.axis_index("tm")
    q = lax.axis_index("chan")
    cross = lax.rem(q + 2, 4)
    sib = q + 1 - 2 * lax.rem(q, 2)
    after = lax.rem(t + 1, ROWS)
    before = lax.rem(t + ROWS - 1, ROWS)
    z = t // 8
    w = t - 8 * z
    inner = [lax.rem(w + j, 8) for j in range(8)]

    def plane(b):
        h = (b + 1) // 2
        zo = 8 + h - 2 * h * lax.rem(b, 2)
        return lax.rem(z + zo, 16) * 8

    def for_peers(act):
        def step(b, carry):
            base = plane(b)
            for j in range(8):
                act(base + inner[j])
            return carry

        lax.fori_loop(0, 15, step, 0)
        for j in range(1, 8):
            act(z * 8 + inner[j])

    pairs = (
        (frames_h, xg.at[q, pl.ds(HALO, COLS)]), (filt_h, filt), (w_in_h, w_in), (taps_h, taps),
        (skip_h, skip), (row_h, row), (tc_h, tcos), (ts_h, tsin), (cc_h, ccos), (cs_h, csin),
        (rowi_h, rowi),
    )
    loads = [pltpu.make_async_copy(a, b, load_sem.at[i]) for i, (a, b) in enumerate(pairs)]
    for e in range(2):
        for n in range(4):
            loads.append(
                pltpu.make_async_copy(
                    w_out_h.at[pl.ds(n * 256 + e * 128, 128)],
                    w_out.at[e, pl.ds(n * 128, 128)],
                    wout_sem.at[4 * e + n],
                )
            )
    for copy in loads[:2]:
        copy.start()

    barrier = pltpu.get_barrier_semaphore()

    def greet(device):
        pl.semaphore_signal(barrier, 1, device_id=device, device_id_type=MESH)

    for_peers(lambda peer: greet({"tm": peer}))
    greet({"chan": cross})
    greet({"chan": sib})
    for n in range(1, 4):
        other = lax.rem(q + n, 4)
        greet({"tm": after, "chan": other})
        greet({"tm": before, "chan": other})

    for copy in loads[2:]:
        copy.start()

    def to_slabs(block_of, cbs, es):
        for e in es:
            for cb in cbs:
                slab[pl.ds(4 * e + cb, ROWS, stride=8), :] = jnp.transpose(block_of(cb, e))

    def pack(send, e):
        def step(i, carry):
            rows = slab[pl.ds(pl.multiple_of(i * LANES, LANES), LANES), :].reshape(16, 8, LANES)
            send[pl.ds(i * 16, 16), 4 * e : 4 * e + 4] = rows[:, 4 * e : 4 * e + 4].astype(BF16)
            return carry

        lax.fori_loop(0, 8, step, 0)

    def unpack(recv, e):
        def step(i, carry):
            rows = recv[pl.ds(i * 16, 16), 4 * e : 4 * e + 4].astype(F32)
            for n in range(4):
                slab[pl.ds(i * LANES + 4 * e + n, 16, stride=8), :] = rows[:, n]
            return carry

        lax.fori_loop(0, 8, step, 0)

    def spread(send, recv, which, e):
        part = pl.ds(4 * e, 4)

        def act(peer):
            pltpu.make_async_remote_copy(
                send.at[peer, part], recv.at[t, part],
                a_s.at[2 * which + e], a_r.at[2 * which + e],
                device_id={"tm": peer}, device_id_type=MESH,
            ).start()

        for_peers(act)
        recv[t, part] = send[t, part]

    def await_recv(recv, which, e):
        part = recv.at[pl.ds(0, PEERS), pl.ds(4 * e, 4)]
        pltpu.make_async_copy(part, part, a_r.at[2 * which + e]).wait()

    def await_send(send, which, e):
        part = send.at[pl.ds(0, PEERS), pl.ds(4 * e, 4)]
        pltpu.make_async_copy(part, part, a_s.at[2 * which + e]).wait()

    loads[1].wait()
    to_slabs(
        lambda cb, e: filt[cb * 128 : cb * 128 + 128, e * 128 : e * 128 + 128].astype(F32),
        range(4), range(2),
    )
    pack(fsend, 0)
    pack(fsend, 1)
    loads[0].wait()
    pl.semaphore_wait(barrier, PEERS + 8)

    def gather_start(src, dst, i, s1, r1, s2, r2):
        made = []
        for peer, s, r in ((cross, s1, r1), (sib, s2, r2)):
            copy = pltpu.make_async_remote_copy(
                src, dst, s.at[i], r.at[i], device_id={"chan": peer}, device_id_type=MESH
            )
            copy.start()
            made.append(copy)
        return made

    def gather_pass(held, i, s3, r3):
        on = pltpu.make_async_remote_copy(
            held, held, s3.at[i], r3.at[i], device_id={"chan": sib}, device_id_type=MESH
        )
        on.start()
        return on

    last = xg.at[q, pl.ds(COLS, HALO)]
    for n in range(4):
        pltpu.make_async_remote_copy(
            last, xg.at[q, pl.ds(0, HALO)], h_s, h_r,
            device_id={"tm": after, "chan": lax.rem(q + n, 4)}, device_id_type=MESH,
        ).start()
    chunk = [pl.ds(HALO + 256 * i, 256) for i in range(2)]
    first = [
        gather_start(xg.at[q, chunk[i]], xg.at[q, chunk[i]], i, over_s, over_r, near_s, near_r)
        for i in range(2)
    ]
    spread(fsend, frecv, 0, 0)
    spread(fsend, frecv, 0, 1)
    loads[2].wait()
    loads[3].wait()
    passed = []
    first[0][0].wait_recv()
    passed.append(gather_pass(xg.at[cross, chunk[0]], 0, pass_s, pass_r))

    def project(low, high):
        for j in range(3):
            total = dot(xg[0, low:high], w_in[j, 0:256])
            for n in range(1, 4):
                total += dot(xg[n, low:high], w_in[j, n * 256 : n * 256 + 256])
            p[low:high, j * 256 : j * 256 + 256] = total.astype(BF16).astype(F32)

    def short(i):
        for base in range(i * 256, i * 256 + 256, 64):
            made = []
            for j in range(3):
                lanes = slice(j * 256, j * 256 + 256)
                made.append(
                    taps[j, 0:1, :] * p[16 + base : 80 + base, lanes]
                    + taps[j, 1:2, :] * p[15 + base : 79 + base, lanes]
                    + taps[j, 2:3, :] * p[14 + base : 78 + base, lanes]
                )
            qf[base : base + 64, :] = made[0]
            sf[base : base + 64, :] = (made[1] * made[2]).astype(BF16).astype(F32)

    edge = xg.at[pl.ds(0, 4), pl.ds(0, HALO)]
    pltpu.make_async_copy(edge, edge, h_r).wait()
    first[0][1].wait_recv()
    passed[0].wait_recv()
    project(0, HALO + 256)
    p[0:HALO, :] = jnp.where(t > 0, p[0:HALO, :], 0.0)
    first[1][0].wait_recv()
    passed.append(gather_pass(xg.at[cross, chunk[1]], 1, pass_s, pass_r))
    block = lambda cb, e: sf[cb * 128 : cb * 128 + 128, e * 128 : e * 128 + 128]
    short(0)
    to_slabs(block, (0, 1), range(2))
    first[1][1].wait_recv()
    passed[1].wait_recv()
    project(HALO + 256, HALO + COLS)
    short(1)
    for e in range(2):
        to_slabs(block, (2, 3), (e,))
        pack(ssend, e)
        spread(ssend, srecv, 1, e)

    for copy in loads[4:]:
        copy.wait()

    def transform(recv, e):
        unpack(recv, e)
        for cb in range(4):
            gmat[:, cb * 128 : cb * 128 + 128] = slab[
                pl.ds(4 * e + cb, ROWS, stride=8), :
            ].astype(BF16)
        both = dot(row[...], gmat[...])
        a, b = both[0:128], both[128:256]
        q2[0:128, :] = (a * tcos[...] + b * tsin[...]).astype(BF16)
        q2[128:256, :] = (b * tcos[...] - a * tsin[...]).astype(BF16)
        xm[...] = dot(q2[...], ccos[...])
        ym[...] = dot(q2[...], csin[...])

    for e in range(2):
        await_recv(frecv, 0, e)
        transform(frecv, e)
        spec[e, 0:128, :] = xm[0:128, :] + ym[128:256, :]
        spec[e, 128:256, :] = xm[128:256, :] - ym[0:128, :]

    for e in range(2):
        await_recv(srecv, 1, e)
        transform(srecv, e)
        sr = xm[0:128, :] + ym[128:256, :]
        si = xm[128:256, :] - ym[0:128, :]
        fr, fi = spec[e, 0:128, :], spec[e, 128:256, :]
        scale = 1.0 / (ROWS * COLS)
        q2[0:128, :] = ((sr * fr - si * fi) * scale).astype(BF16)
        q2[128:256, :] = ((sr * fi + si * fr) * scale).astype(BF16)
        xm[...] = dot(q2[...], ccos[...])
        ym[...] = dot(q2[...], csin[...])
        br = xm[0:128, :] - ym[128:256, :]
        bi = ym[0:128, :] + xm[128:256, :]
        bstack[0:128, :] = (br * tcos[...] - bi * tsin[...]).astype(BF16)
        bstack[128:256, :] = (br * tsin[...] + bi * tcos[...]).astype(BF16)
        conv = dot(rowi[...], bstack[...])
        for cb in range(4):
            slab[pl.ds(4 * e + cb, ROWS, stride=8), :] = conv[:, cb * 128 : cb * 128 + 128]
        pack(csend, e)
        spread(csend, crecv, 2, e)

    second = []
    for e in range(2):
        await_recv(crecv, 2, e)
        unpack(crecv, e)
        lanes = slice(e * 128, e * 128 + 128)
        for cb in range(4):
            rows = slice(cb * 128, cb * 128 + 128)
            conv = jnp.transpose(slab[pl.ds(4 * e + cb, ROWS, stride=8), :])
            gated = qf[rows, lanes] * (conv + skip[:, lanes] * sf[rows, lanes])
            gbuf[e, rows, :] = gated.astype(BF16)
        place = pl.ds(pl.multiple_of(q * 128, 128), 128)
        second.append(
            gather_start(gbuf.at[e], gg.at[e, :, place], e, gover_s, gover_r, gnear_s, gnear_r)
        )
        gg[e, :, place] = gbuf[e]

    onward = []
    for e in range(2):
        second[e][0].wait_recv()
        held = gg.at[e, :, pl.ds(pl.multiple_of(cross * 128, 128), 128)]
        onward.append(gather_pass(held, e, gpass_s, gpass_r))
        second[e][1].wait_recv()
        onward[e].wait_recv()
        total = dot(gg[e], w_out[e])
        if e == 0:
            acc[...] = total + xg[q, HALO : HALO + COLS].astype(F32)
        else:
            out[...] = (acc[...] + total).astype(BF16)

    for e in range(2):
        await_send(fsend, 0, e)
        await_send(ssend, 1, e)
        await_send(csend, 2, e)
    pltpu.make_async_copy(edge, edge, h_s).wait()
    for copies in first + second:
        for copy in copies:
            copy.wait_send()
    for copy in passed + onward:
        copy.wait_send()


def per_device(frames, w_in, short_taps, filter_taps, skip_gain, w_out):
    vmem = pl.BlockSpec(memory_space=pltpu.VMEM)
    hbm = pl.BlockSpec(memory_space=pl.ANY)
    dma = pltpu.SemaphoreType.DMA
    row, rowi, tc, ts, cc, cs = tables()
    slabs = pltpu.VMEM((ROWS, 8, LANES), BF16)
    scratch = [
        pltpu.VMEM((3, 3, 256), F32), pltpu.VMEM((1, 256), F32),
        pltpu.VMEM((3, 1024, 256), BF16), pltpu.VMEM((2, 512, 256), BF16),
        pltpu.VMEM((256, 128), BF16), pltpu.VMEM((128, 256), BF16),
        pltpu.VMEM((128, 512), F32), pltpu.VMEM((128, 512), F32),
        pltpu.VMEM((512, 512), BF16), pltpu.VMEM((512, 512), BF16),
        pltpu.VMEM((4, HALO + COLS, 256), BF16),
        pltpu.VMEM((512, 256), BF16),
        pltpu.VMEM((HALO + COLS, 768), F32),
        pltpu.VMEM((512, 256), F32), pltpu.VMEM((512, 256), F32),
        pltpu.VMEM((1024, 128), F32),
        slabs, slabs, slabs, slabs, slabs, slabs,
        pltpu.VMEM((2, 512, 128), BF16),
        pltpu.VMEM((2, 512, 512), BF16),
        pltpu.VMEM((128, 512), BF16),
        pltpu.VMEM((256, 512), BF16),
        pltpu.VMEM((2, 256, 512), F32),
        pltpu.VMEM((256, 512), F32), pltpu.VMEM((256, 512), F32),
        pltpu.VMEM((256, 512), BF16),
        pltpu.VMEM((512, 256), F32),
        dma((11,)), dma((8,)),
    ] + [dma((2,))] * 12 + [dma((6,)), dma((6,)), dma, dma]
    return pl.pallas_call(
        kernel,
        out_shape=jax.ShapeDtypeStruct(frames.shape, BF16),
        in_specs=[hbm] * 12,
        out_specs=vmem,
        scratch_shapes=scratch,
        name="hyena",
        compiler_params=pltpu.CompilerParams(
            collective_id=0, has_side_effects=True, vmem_limit_bytes=60 << 20
        ),
    )(frames, filter_taps, short_taps, skip_gain.reshape(1, -1), w_in, w_out, row, rowi, tc, ts, cc, cs)


def solution(mesh):
    return jax.shard_map(
        per_device,
        mesh=mesh,
        in_specs=(
            P("tm", "chan"),
            P(None, None, "chan"),
            P(None, None, "chan"),
            P("tm", "chan"),
            P("chan"),
            P(None, "chan"),
        ),
        out_specs=P("tm", "chan"),
        check_vma=False,
    )
```

profile of v0, /device:TPU:1, one launch (start us, length us, event | category | flops | bytes accessed | tf_op | source)
XLA Modules:
  0.0 69.7 jit_solution(6973243481466993998)
XLA Ops:
  0.0 68.0 %hyena.1 = bf16[512,256]{1,0:T(8,128)(2,1)} custom-call(bf16[512,256]{1,0:T(8,128)(2,1)} %frames_h.1, bf16[512,256]{1,0:T(8,128)(2,1)} %filt_h.1, f32[3,3,256]{2,1,0:T(4,128)} %taps_h.1, f32[1,256]{1,0:T(1,128)} %bitcast.1, bf16[3,1024,256]{2,1,0:T(8,128)(2,1)} %w_in_h.1, bf16[1024,256]{1,0:T(8,128)(2,1)} %w_out_h.1, bf16[256,128]{1,0:T(8,128)(2,1)} %constant.12.clone.row_h, ...), custom_call_target="tpu_custom_call" | custom-call | tf_op jit(solution)/shard_map/hyena/pallas_call | solution.py:354
  68.0 1.7 %copy.14 = bf16[512,256]{1,0:T(8,128)(2,1)} copy(bf16[512,256]{1,0:T(8,128)(2,1)} %hyena.1) | data formatting | bytes 524288
where the time goes:
time: 69.8 us; the launch traced here: 69.7 us
  Pallas kernels  68 us (97%)
  local copies, waits for them, and re-layouts  1.67 us (2%)
    pallas_call x1, Pallas kernels, per_device(): pl.pallas_call(kernel, out_shape=jax.ShapeDtypeStruct(frames.shape, BF16)...  68 us
    unnamed x1, local copies, waits for them, and re-layouts  1.67 us

commit v1 on v0

--- a/solution.py
+++ b/solution.py
@@ -65,16 +65,17 @@
         zo = 8 + h - 2 * h * lax.rem(b, 2)
         return lax.rem(z + zo, 16) * 8
 
-    def for_peers(act):
+    def for_peers(act, chosen=range(8)):
         def step(b, carry):
             base = plane(b)
-            for j in range(8):
+            for j in chosen:
                 act(base + inner[j])
             return carry
 
         lax.fori_loop(0, 15, step, 0)
-        for j in range(1, 8):
-            act(z * 8 + inner[j])
+        for j in chosen:
+            if j > 0:
+                act(z * 8 + inner[j])
 
     pairs = (
         (frames_h, xg.at[q, pl.ds(HALO, COLS)]), (filt_h, filt), (w_in_h, w_in), (taps_h, taps),
@@ -123,35 +124,32 @@
 
         lax.fori_loop(0, 8, step, 0)
 
-    def unpack(recv, e):
+    def unpack(recv, e, low=0, high=4):
         def step(i, carry):
-            rows = recv[pl.ds(i * 16, 16), 4 * e : 4 * e + 4].astype(F32)
-            for n in range(4):
-                slab[pl.ds(i * LANES + 4 * e + n, 16, stride=8), :] = rows[:, n]
+            rows = recv[pl.ds(i * 16, 16), 4 * e + low : 4 * e + high].astype(F32)
+            for n in range(high - low):
+                slab[pl.ds(i * LANES + 4 * e + low + n, 16, stride=8), :] = rows[:, n]
             return carry
 
         lax.fori_loop(0, 8, step, 0)
 
-    def spread(send, recv, which, e):
-        part = pl.ds(4 * e, 4)
-
+    def spread(send, recv, which, part, walk=for_peers):
         def act(peer):
             pltpu.make_async_remote_copy(
-                send.at[peer, part], recv.at[t, part],
-                a_s.at[2 * which + e], a_r.at[2 * which + e],
+                send.at[peer, part], recv.at[t, part], a_s.at[which], a_r.at[which],
                 device_id={"tm": peer}, device_id_type=MESH,
             ).start()
 
-        for_peers(act)
-        recv[t, part] = send[t, part]
-
-    def await_recv(recv, which, e):
-        part = recv.at[pl.ds(0, PEERS), pl.ds(4 * e, 4)]
-        pltpu.make_async_copy(part, part, a_r.at[2 * which + e]).wait()
-
-    def await_send(send, which, e):
-        part = send.at[pl.ds(0, PEERS), pl.ds(4 * e, 4)]
-        pltpu.make_async_copy(part, part, a_s.at[2 * which + e]).wait()
+        walk(act)
+
+    def await_all(held, part, sem):
+        some = held.at[pl.ds(0, PEERS), part]
+        pltpu.make_async_copy(some, some, sem).wait()
+
+    WHOLE = pl.ds(0, 8)
+    HALF = (pl.ds(0, 4), pl.ds(4, 4))
+    PIECES = ((0, 0, 4), (1, 0, 4))
+    PARTS = [pl.ds(4 * e + low, high - low) for e, low, high in PIECES]
 
     loads[1].wait()
     to_slabs(
@@ -191,20 +189,14 @@
         gather_start(xg.at[q, chunk[i]], xg.at[q, chunk[i]], i, over_s, over_r, near_s, near_r)
         for i in range(2)
     ]
-    spread(fsend, frecv, 0, 0)
-    spread(fsend, frecv, 0, 1)
-    loads[2].wait()
-    loads[3].wait()
+    spread(fsend, frecv, 0, WHOLE, lambda act: for_peers(act, (0, 2, 4, 6)))
+    frecv[t] = fsend[t]
     passed = []
     first[0][0].wait_recv()
     passed.append(gather_pass(xg.at[cross, chunk[0]], 0, pass_s, pass_r))
-
-    def project(low, high):
-        for j in range(3):
-            total = dot(xg[0, low:high], w_in[j, 0:256])
-            for n in range(1, 4):
-                total += dot(xg[n, low:high], w_in[j, n * 256 : n * 256 + 256])
-            p[low:high, j * 256 : j * 256 + 256] = total.astype(BF16).astype(F32)
+    spread(fsend, frecv, 0, WHOLE, lambda act: for_peers(act, (1, 3, 5, 7)))
+    loads[2].wait()
+    loads[3].wait()
 
     def short(i):
         for base in range(i * 256, i * 256 + 256, 64):
@@ -220,24 +212,44 @@
             sf[base : base + 64, :] = (made[1] * made[2]).astype(BF16).astype(F32)
 
     edge = xg.at[pl.ds(0, 4), pl.ds(0, HALO)]
+    diagonal = lax.rem(sib + 2, 4)
+    block = lambda cb, e: sf[cb * 128 : cb * 128 + 128, e * 128 : e * 128 + 128]
+    spans = ((0, HALO + 256), (HALO + 256, HALO + COLS))
+
+    def add_product(i, n, state):
+        low, high = spans[i]
+        held = xg[n, low:high]
+        for j in range(3):
+            lanes = slice(j * 256, j * 256 + 256)
+            total = dot(held, w_in[j, pl.ds(pl.multiple_of(n * 256, 256), 256)])
+            if state > 0:
+                total += p[low:high, lanes]
+            if state == 2:
+                total = total.astype(BF16).astype(F32)
+            p[low:high, lanes] = total
+
     pltpu.make_async_copy(edge, edge, h_r).wait()
-    first[0][1].wait_recv()
-    passed[0].wait_recv()
-    project(0, HALO + 256)
-    p[0:HALO, :] = jnp.where(t > 0, p[0:HALO, :], 0.0)
-    first[1][0].wait_recv()
-    passed.append(gather_pass(xg.at[cross, chunk[1]], 1, pass_s, pass_r))
-    block = lambda cb, e: sf[cb * 128 : cb * 128 + 128, e * 128 : e * 128 + 128]
-    short(0)
-    to_slabs(block, (0, 1), range(2))
-    first[1][1].wait_recv()
-    passed[1].wait_recv()
-    project(HALO + 256, HALO + COLS)
+    for i in range(2):
+        add_product(i, q, 0)
+        first[i][1].wait_recv()
+        add_product(i, sib, 1)
+        if i == 1:
+            first[1][0].wait_recv()
+            passed.append(gather_pass(xg.at[cross, chunk[1]], 1, pass_s, pass_r))
+        add_product(i, cross, 1)
+        if i == 1:
+            short(0)
+            to_slabs(block, (0, 1), range(2))
+        passed[i].wait_recv()
+        add_product(i, diagonal, 2)
+        if i == 0:
+            p[0:HALO, :] = jnp.where(t > 0, p[0:HALO, :], 0.0)
     short(1)
     for e in range(2):
         to_slabs(block, (2, 3), (e,))
         pack(ssend, e)
-        spread(ssend, srecv, 1, e)
+        spread(ssend, srecv, 1 + e, HALF[e])
+        srecv[t, HALF[e]] = ssend[t, HALF[e]]
 
     for copy in loads[4:]:
         copy.wait()
@@ -255,14 +267,14 @@
         xm[...] = dot(q2[...], ccos[...])
         ym[...] = dot(q2[...], csin[...])
 
+    await_all(frecv, WHOLE, a_r.at[0])
     for e in range(2):
-        await_recv(frecv, 0, e)
         transform(frecv, e)
         spec[e, 0:128, :] = xm[0:128, :] + ym[128:256, :]
         spec[e, 128:256, :] = xm[128:256, :] - ym[0:128, :]
 
     for e in range(2):
-        await_recv(srecv, 1, e)
+        await_all(srecv, HALF[e], a_r.at[1 + e])
         transform(srecv, e)
         sr = xm[0:128, :] + ym[128:256, :]
         si = xm[128:256, :] - ym[0:128, :]
@@ -280,41 +292,60 @@
         for cb in range(4):
             slab[pl.ds(4 * e + cb, ROWS, stride=8), :] = conv[:, cb * 128 : cb * 128 + 128]
         pack(csend, e)
-        spread(csend, crecv, 2, e)
-
-    second = []
-    for e in range(2):
-        await_recv(crecv, 2, e)
-        unpack(crecv, e)
+        for i, piece in enumerate(PIECES):
+            if piece[0] == e:
+                spread(csend, crecv, 3 + i, PARTS[i])
+        crecv[t, HALF[e]] = csend[t, HALF[e]]
+
+    second, onward = [], []
+    place = pl.ds(pl.multiple_of(q * 128, 128), 128)
+    cross_place = pl.ds(pl.multiple_of(cross * 128, 128), 128)
+
+    def returned(i):
+        e, low, high = PIECES[i]
+        await_all(crecv, PARTS[i], a_r.at[3 + i])
+        unpack(crecv, e, low, high)
         lanes = slice(e * 128, e * 128 + 128)
-        for cb in range(4):
+        for cb in range(low, high):
             rows = slice(cb * 128, cb * 128 + 128)
             conv = jnp.transpose(slab[pl.ds(4 * e + cb, ROWS, stride=8), :])
             gated = qf[rows, lanes] * (conv + skip[:, lanes] * sf[rows, lanes])
             gbuf[e, rows, :] = gated.astype(BF16)
-        place = pl.ds(pl.multiple_of(q * 128, 128), 128)
+        rows = pl.ds(low * 128, (high - low) * 128)
         second.append(
-            gather_start(gbuf.at[e], gg.at[e, :, place], e, gover_s, gover_r, gnear_s, gnear_r)
+            gather_start(
+                gbuf.at[e, rows], gg.at[e, rows, place], i, gover_s, gover_r, gnear_s, gnear_r
+            )
         )
-        gg[e, :, place] = gbuf[e]
-
-    onward = []
+        gg[e, rows, place] = gbuf[e, rows]
+
+    def forward(i):
+        e, low, high = PIECES[i]
+        second[i][0].wait_recv()
+        held = gg.at[e, pl.ds(low * 128, (high - low) * 128), cross_place]
+        onward.append(gather_pass(held, i, gpass_s, gpass_r))
+
+    def mixed(i):
+        e, low, high = PIECES[i]
+        rows = slice(low * 128, high * 128)
+        second[i][1].wait_recv()
+        onward[i].wait_recv()
+        return rows, dot(gg[e, rows], w_out[e])
+
+    returned(0)
+    forward(0)
+    returned(1)
+    rows, total = mixed(0)
+    acc[rows, :] = total + xg[q, HALO : HALO + COLS].astype(F32)
+    forward(1)
+    rows, total = mixed(1)
+    out[rows, :] = (acc[rows, :] + total).astype(BF16)
+
+    await_all(fsend, WHOLE, a_s.at[0])
     for e in range(2):
-        second[e][0].wait_recv()
-        held = gg.at[e, :, pl.ds(pl.multiple_of(cross * 128, 128), 128)]
-        onward.append(gather_pass(held, e, gpass_s, gpass_r))
-        second[e][1].wait_recv()
-        onward[e].wait_recv()
-        total = dot(gg[e], w_out[e])
-        if e == 0:
-            acc[...] = total + xg[q, HALO : HALO + COLS].astype(F32)
-        else:
-            out[...] = (acc[...] + total).astype(BF16)
-
-    for e in range(2):
-        await_send(fsend, 0, e)
-        await_send(ssend, 1, e)
-        await_send(csend, 2, e)
+        await_all(ssend, HALF[e], a_s.at[1 + e])
+    for i in range(2):
+        await_all(csend, PARTS[i], a_s.at[3 + i])
     pltpu.make_async_copy(edge, edge, h_s).wait()
     for copies in first + second:
         for copy in copies:
@@ -328,6 +359,10 @@
     hbm = pl.BlockSpec(memory_space=pl.ANY)
     dma = pltpu.SemaphoreType.DMA
     row, rowi, tc, ts, cc, cs = tables()
+    operands = (
+        frames, filter_taps, short_taps, skip_gain.reshape(1, -1), w_in, w_out,
+        row, rowi, tc, ts, cc, cs,
+    )
     slabs = pltpu.VMEM((ROWS, 8, LANES), BF16)
     scratch = [
         pltpu.VMEM((3, 3, 256), F32), pltpu.VMEM((1, 256), F32),
@@ -350,7 +385,7 @@
         pltpu.VMEM((256, 512), BF16),
         pltpu.VMEM((512, 256), F32),
         dma((11,)), dma((8,)),
-    ] + [dma((2,))] * 12 + [dma((6,)), dma((6,)), dma, dma]
+    ] + [dma((2,))] * 6 + [dma((3,))] * 6 + [dma((6,)), dma((6,)), dma, dma]
     return pl.pallas_call(
         kernel,
         out_shape=jax.ShapeDtypeStruct(frames.shape, BF16),
@@ -359,9 +394,9 @@
         scratch_shapes=scratch,
         name="hyena",
         compiler_params=pltpu.CompilerParams(
-            collective_id=0, has_side_effects=True, vmem_limit_bytes=60 << 20
+            collective_id=0, has_side_effects=True, vmem_limit_bytes=30 << 20
         ),
-    )(frames, filter_taps, short_taps, skip_gain.reshape(1, -1), w_in, w_out, row, rowi, tc, ts, cc, cs)
+    )(*[pltpu.with_memory_space_constraint(v, pltpu.HBM) for v in operands])
 
 
 def solution(mesh):

time: 69.8 us -> 66.6 us (0.954)
  Pallas kernels: 68 us -> 65.7 us
  local copies, waits for them, and re-layouts: 1.67 us -> 0.71 us
    pallas_call x1, Pallas kernels: 68 us -> 65.7 us  [per_device(): pl.pallas_call(kernel, out_shape=jax.ShapeDtypeStruct(frames.shape, BF16)...]
    unnamed x1, local copies, waits for them, and re-layouts: 1.67 us -> 0.71 us
where the time goes in v1:
time: 66.6 us; the launch traced here: 66.4 us
  Pallas kernels  65.7 us (99%)
  local copies, waits for them, and re-layouts  0.71 us (1%)
    pallas_call x1, Pallas kernels, per_device(): pl.pallas_call(kernel, out_shape=jax.ShapeDtypeStruct(frames.shape, BF16)...  65.7 us

profile of v1, /device:TPU:1, one launch (start us, length us, event | category | flops | bytes accessed | tf_op | source)
XLA Modules:
  0.0 66.4 jit_solution(13391080340971388827)
XLA Ops:
  0.0 65.7 %hyena.1 = bf16[512,256]{1,0:T(8,128)(2,1)S(1)} custom-call(bf16[512,256]{1,0:T(8,128)(2,1)} %frames_h.1, bf16[512,256]{1,0:T(8,128)(2,1)} %filt_h.1, f32[3,3,256]{2,1,0:T(4,128)} %taps_h.1, f32[1,256]{1,0:T(1,128)} %bitcast.1, bf16[3,1024,256]{2,1,0:T(8,128)(2,1)} %w_in_h.1, bf16[1024,256]{1,0:T(8,128)(2,1)} %w_out_h.1, ...), custom_call_target="tpu_custom_call" | custom-call | tf_op jit(solution)/shard_map/hyena/pallas_call | solution.py:389
  65.7 0.7 %copy.14 = bf16[512,256]{1,0:T(8,128)(2,1)} copy(bf16[512,256]{1,0:T(8,128)(2,1)S(1)} %hyena.1) | data formatting | bytes 524288

commit v2 on v1

--- a/solution.py
+++ b/solution.py
@@ -14,6 +14,7 @@
 CHANS = 256
 PEERS = ROWS - 1
 LANES = 128
+EARLY = 2
 HALO = 16
 F32 = jnp.float32
 BF16 = jnp.bfloat16
@@ -48,7 +49,7 @@
     xg, filt, p, qf, sf, slab, fsend, frecv, ssend, srecv, csend, crecv,
     gbuf, gg, gmat, q2, spec, xm, ym, bstack, acc,
     load_sem, wout_sem, over_s, over_r, near_s, near_r, pass_s, pass_r,
-    gover_s, gover_r, gnear_s, gnear_r, gpass_s, gpass_r, a_s, a_r, h_s, h_r,
+    gover_s, gover_r, gnear_s, gnear_r, gpass_s, gpass_r, a_s, a_r, h_s, h_r, last_s,
 ):
     t = lax.axis_index("tm")
     q = lax.axis_index("chan")
@@ -76,6 +77,28 @@
         for j in chosen:
             if j > 0:
                 act(z * 8 + inner[j])
+
+    def for_peers_early(act):
+        for other in range(EARLY):
+
+            @pl.when(z != other)
+            def _():
+                for j in range(8):
+                    act(other * 8 + inner[j])
+
+        def step(b, carry):
+            base = plane(b)
+
+            @pl.when(base >= EARLY * 8)
+            def _():
+                for j in range(8):
+                    act(base + inner[j])
+
+            return carry
+
+        lax.fori_loop(0, 15, step, 0)
+        for j in range(1, 8):
+            act(z * 8 + inner[j])
 
     pairs = (
         (frames_h, xg.at[q, pl.ds(HALO, COLS)]), (filt_h, filt), (w_in_h, w_in), (taps_h, taps),
@@ -189,12 +212,12 @@
         gather_start(xg.at[q, chunk[i]], xg.at[q, chunk[i]], i, over_s, over_r, near_s, near_r)
         for i in range(2)
     ]
-    spread(fsend, frecv, 0, WHOLE, lambda act: for_peers(act, (0, 2, 4, 6)))
+    spread(fsend, frecv, 0, WHOLE, lambda act: for_peers(act, (0, 2, 4, 6, 1)))
     frecv[t] = fsend[t]
     passed = []
     first[0][0].wait_recv()
     passed.append(gather_pass(xg.at[cross, chunk[0]], 0, pass_s, pass_r))
-    spread(fsend, frecv, 0, WHOLE, lambda act: for_peers(act, (1, 3, 5, 7)))
+    spread(fsend, frecv, 0, WHOLE, lambda act: for_peers(act, (3, 5, 7)))
     loads[2].wait()
     loads[3].wait()
 
@@ -294,12 +317,14 @@
         pack(csend, e)
         for i, piece in enumerate(PIECES):
             if piece[0] == e:
-                spread(csend, crecv, 3 + i, PARTS[i])
+                walk = for_peers_early if e == 1 else for_peers
+                spread(csend, crecv, 3 + i, PARTS[i], walk)
         crecv[t, HALF[e]] = csend[t, HALF[e]]
 
     second, onward = [], []
     place = pl.ds(pl.multiple_of(q * 128, 128), 128)
     cross_place = pl.ds(pl.multiple_of(cross * 128, 128), 128)
+    sib_place = pl.ds(pl.multiple_of(sib * 128, 128), 128)
 
     def returned(i):
         e, low, high = PIECES[i]
@@ -337,8 +362,29 @@
     returned(1)
     rows, total = mixed(0)
     acc[rows, :] = total + xg[q, HALO : HALO + COLS].astype(F32)
-    forward(1)
-    rows, total = mixed(1)
+    second[1][0].wait_recv()
+    relays = [
+        pltpu.make_async_remote_copy(
+            gg.at[1, :, source], gg.at[1, :, source], sem, gpass_r.at[1],
+            device_id={"chan": peer}, device_id_type=MESH,
+        )
+        for source, sem, peer in (
+            (cross_place, gpass_s.at[1], sib), (sib_place, last_s, cross)
+        )
+    ]
+
+    @pl.when(lax.rem(q, 2) == 1)
+    def _():
+        relays[0].start()
+        second[1][1].wait_recv()
+        relays[1].start()
+
+    @pl.when(lax.rem(q, 2) == 0)
+    def _():
+        second[1][1].wait_recv()
+
+    relays[0].wait_recv()
+    rows, total = slice(0, 512), dot(gg[1], w_out[1])
     out[rows, :] = (acc[rows, :] + total).astype(BF16)
 
     await_all(fsend, WHOLE, a_s.at[0])
@@ -352,6 +398,11 @@
             copy.wait_send()
     for copy in passed + onward:
         copy.wait_send()
+
+    @pl.when(lax.rem(q, 2) == 1)
+    def _():
+        for copy in relays:
+            copy.wait_send()
 
 
 def per_device(frames, w_in, short_taps, filter_taps, skip_gain, w_out):
@@ -385,7 +436,7 @@
         pltpu.VMEM((256, 512), BF16),
         pltpu.VMEM((512, 256), F32),
         dma((11,)), dma((8,)),
-    ] + [dma((2,))] * 6 + [dma((3,))] * 6 + [dma((6,)), dma((6,)), dma, dma]
+    ] + [dma((2,))] * 6 + [dma((3,))] * 6 + [dma((6,)), dma((6,)), dma, dma, dma]
     return pl.pallas_call(
         kernel,
         out_shape=jax.ShapeDtypeStruct(frames.shape, BF16),

time: 66.6 us -> 65.9 us (0.989)
  no operation moved by 1% of the time
where the time goes in v2:
time: 65.9 us; the launch traced here: 65.8 us
  Pallas kernels  65.1 us (99%)
  local copies, waits for them, and re-layouts  0.71 us (1%)
    pallas_call x1, Pallas kernels, per_device(): pl.pallas_call(kernel, out_shape=jax.ShapeDtypeStruct(frames.shape, BF16)...  65.1 us

profile of v2, /device:TPU:1, one launch (start us, length us, event | category | flops | bytes accessed | tf_op | source)
XLA Modules:
  0.0 65.8 jit_solution(15782082275684132231)
XLA Ops:
  0.0 65.1 %hyena.1 = bf16[512,256]{1,0:T(8,128)(2,1)S(1)} custom-call(bf16[512,256]{1,0:T(8,128)(2,1)} %frames_h.1, bf16[512,256]{1,0:T(8,128)(2,1)} %filt_h.1, f32[3,3,256]{2,1,0:T(4,128)} %taps_h.1, f32[1,256]{1,0:T(1,128)} %bitcast.1, bf16[3,1024,256]{2,1,0:T(8,128)(2,1)} %w_in_h.1, bf16[1024,256]{1,0:T(8,128)(2,1)} %w_out_h.1, ...), custom_call_target="tpu_custom_call" | custom-call | tf_op jit(solution)/shard_map/hyena/pallas_call | solution.py:440
  65.1 0.7 %copy.14 = bf16[512,256]{1,0:T(8,128)(2,1)} copy(bf16[512,256]{1,0:T(8,128)(2,1)S(1)} %hyena.1) | data formatting | bytes 524288
